TPU v7x, 32 devices: a whole 2x2x4 slice. The times are simulated.
32 devices in a mesh: blk: 8 (over z, core), bond: 4 (over y, x).
Axes of the slice: x: 2, y: 2, z: 4, core: 2. Of those that a mesh axis runs over, the one named last changes fastest.
Arguments:
- iso: bfloat16 [8, 256, 256, 256], P('blk', None, 'bond'), may hold values from -0.03125 to 0.03125
- edge_left: bfloat16 [8, 256, 256], P('blk'), may hold values from -0.375 to 0.375
- edge_right: bfloat16 [8, 256, 256], P('blk'), may hold values from -0.375 to 0.375
- coupling: float32 [8, 256, 256], P('blk'), may hold values from -0.25 to 0.25
Outputs:
- iso_out: bfloat16 [8, 256, 256, 256], P('blk', None, 'bond')
- top_env: float32 [8, 256, 256], P('blk')
All inputs are finite; a program needn't handle non-finite values.
Results may differ from a plain program's by a relative error of at most 0.00105.
The roundings to bfloat16 on the way count: a program that leaves them out, or rounds other values in their place, can miss the bound.
Values may be sent and summed in bfloat16 or wider, within the bound.
A program may use at most 128 MiB of HBM per device.

v0:
```python
import jax
import jax.numpy as jnp
from jax import lax
from jax.experimental import pallas as pl
from jax.experimental.pallas import tpu as pltpu
from jax.sharding import PartitionSpec as P

NEWTON = 2
CHUNK = 16
GROUP = 4
TAIL = 16

highest = lax.Precision.HIGHEST
f32 = jnp.float32
bf16 = jnp.bfloat16


def shifted(block, axis, distance):
    devices = range(lax.axis_size(axis))
    route = [((i - distance) % len(devices), i) for i in devices]
    return lax.ppermute(block, axis, route)


def partner_2(block, axis, stride):
    count = lax.axis_size(axis)
    route = []
    for low in range(count):
        high = low | 1 << stride
        if high != low and high < count:
            route += [(low, high), (high, low)]
    return lax.ppermute(block, axis, route)


def mm(a, b):
    return jnp.dot(a, b, preferred_element_type=f32)


def ascend_kernel(iso_ref, edges_ref, rows_ref, total_ref):
    @pl.when(pl.program_id(0) == 0)
    def _():
        total_ref[...] = jnp.zeros_like(total_ref)

    chi = iso_ref.shape[0]
    rows_ref[...] = jnp.transpose(iso_ref[...], (1, 0, 2))

    def step(g, carry):
        mats = [rows_ref[g * GROUP + j] for j in range(GROUP)]
        turned = jnp.concatenate(mats, axis=0).T
        mapped = [mm(edges_ref[...], one) for one in mats]
        for k in range(2):
            both = jnp.concatenate([part[k * chi : (k + 1) * chi] for part in mapped], axis=0)
            high = both.astype(bf16)
            low = (both - high.astype(f32)).astype(bf16)
            total_ref[k] += mm(turned, high) + mm(turned, low)
        return carry

    lax.fori_loop(0, rows_ref.shape[0] // GROUP, step, 0, unroll=2)


def gram_kernel(rows_ref, mix_ref, self_ref, cross_ref, plain_ref):
    @pl.when(pl.program_id(0) == 0)
    def _():
        for ref in (self_ref, cross_ref, plain_ref):
            ref[...] = jnp.zeros_like(ref)

    def step(g, carry):
        mats = [rows_ref[g * GROUP + j] for j in range(GROUP)]
        rows = jnp.concatenate(mats, axis=0)
        moved = jnp.concatenate([mm(mix_ref[...], one).astype(bf16) for one in mats], axis=0)
        turned = moved.T
        self_ref[...] += mm(turned, moved)
        cross_ref[...] += mm(turned, rows)
        plain_ref[...] += mm(rows.T, rows)
        return carry

    lax.fori_loop(0, rows_ref.shape[0] // GROUP, step, 0, unroll=2)


def exact(a, b):
    return jnp.dot(a, b, precision=highest, preferred_element_type=f32)


def diagonal(shape):
    return lax.broadcasted_iota(jnp.int32, shape, 0) == lax.broadcasted_iota(jnp.int32, shape, 1)


def join_kernel(self_ref, cross_ref, plain_ref, top_ref, packed_ref):
    chi = self_ref.shape[0]
    top = top_ref[...].astype(f32)
    half = exact(cross_ref[...] + 0.5 * exact(top.T, plain_ref[...]), top)
    gram = self_ref[...] + half + half.T
    packed_ref[0:chi, :] = gram.astype(bf16)
    trace = jnp.sum(jnp.where(diagonal(gram.shape), gram, 0.0), keepdims=True)
    left = jnp.broadcast_to(trace, (TAIL, chi))
    place = lax.broadcasted_iota(jnp.int32, (TAIL, chi), 0)
    tail = jnp.zeros((TAIL, chi), f32)
    for row in range(3):
        head = left.astype(bf16).astype(f32)
        tail = jnp.where(place == row, head, tail)
        left = left - head
    packed_ref[chi : chi + TAIL, :] = tail.astype(bf16)


def update_kernel(rows_ref, mix_ref, top_ref, packed_ref, out_ref, held_ref, rest_ref, mean_ref):
    @pl.when(pl.program_id(0) == 0)
    def _():
        chi = mix_ref.shape[0]
        packed = packed_ref[0].astype(f32)
        for rank in range(1, packed_ref.shape[0]):
            packed = packed + packed_ref[rank].astype(f32)
        squares = jnp.sum(packed[chi:], axis=0, keepdims=True)
        scale = lax.rsqrt(squares + 1e-06)
        first_gram = packed[:chi] * (scale * scale)
        gram = first_gram
        eye = diagonal(gram.shape).astype(f32)
        total = eye
        for newton_step in range(NEWTON):
            step = 1.5 * eye - 0.5 * gram
            total = step if newton_step == 0 else exact(total, step)
            if newton_step + 1 < NEWTON:
                gram = exact(exact(step, gram), step)
        energy = jnp.sum(first_gram * eye, keepdims=True)
        mean = jnp.sum(first_gram * total, keepdims=True) / jnp.maximum(energy, 1e-30)
        rest_ref[...] = ((total - mean * eye) * scale).astype(bf16)
        mean_ref[...] = mean * scale

    mean = mean_ref[...]

    def step(g, carry):
        mats = [rows_ref[g * GROUP + j] for j in range(GROUP)]
        rows = jnp.concatenate(mats, axis=0)
        moved = jnp.concatenate([mm(mix_ref[...], one) for one in mats], axis=0)
        grad = moved + mm(rows, top_ref[...])
        done = (mean * grad + mm(grad.astype(bf16), rest_ref[...])).astype(bf16)
        held_ref[pl.ds(g * GROUP, GROUP)] = done.reshape(GROUP, *mix_ref.shape)
        return carry

    lax.fori_loop(0, rows_ref.shape[0] // GROUP, step, 0, unroll=2)
    out_ref[...] = jnp.transpose(held_ref[...], (1, 0, 2))


def whole(shape):
    return pl.BlockSpec(shape, lambda i: (0,) * len(shape))


def body(iso, edge_left, edge_right, coupling):
    iso = iso[0]
    chi, depth, _ = iso.shape
    chunk = CHUNK if depth % CHUNK == 0 else depth
    steps = depth // chunk
    square = (chi, chi)
    iso_spec = pl.BlockSpec((chi, chunk, chi), lambda i: (0, i, 0))
    rows_spec = pl.BlockSpec((chunk, chi, chi), lambda i: (i, 0, 0))
    params = pltpu.CompilerParams(
        dimension_semantics=("arbitrary",), vmem_limit_bytes=48 * 1024 * 1024
    )
    work = 2 * depth * chi**3
    edges = jnp.concatenate([edge_left[0], edge_right[0]], axis=0)
    rows, partial_value = pl.pallas_call(
        ascend_kernel,
        grid=(steps,),
        in_specs=[iso_spec, whole((2 * chi, chi))],
        out_specs=[rows_spec, whole((2, *square))],
        out_shape=[
            jax.ShapeDtypeStruct((depth, *square), bf16),
            jax.ShapeDtypeStruct((2, *square), f32),
        ],
        compiler_params=params,
        cost_estimate=pl.CostEstimate(flops=6 * work, bytes_accessed=4 * iso.size, transcendentals=0),
        name="ascend",
    )(iso, edges)
    ranks = lax.axis_size("bond")
    pieces = partial_value.reshape(ranks, -1, chi)
    pieces = lax.all_to_all(pieces, "bond", 0, 0, tiled=True)
    piece = jnp.sum(pieces, axis=0).astype(bf16)
    bounds = lax.all_gather(piece, "bond", axis=0, tiled=True).reshape(2, *square)
    own_left = bounds[0]
    own_right = bounds[1]
    from_left = shifted(own_right, "blk", 1)
    from_right = shifted(own_left, "blk", -1)
    mixed_op = edge_left[0].astype(f32) + from_left.astype(f32) + from_right.astype(f32)
    mixed_op = mixed_op.astype(bf16)
    environ = own_left.astype(f32) + own_right.astype(f32)
    couple_mat = coupling[0]
    levels = lax.axis_size("blk").bit_length() - 1
    for level_idx in range(levels):
        if level_idx == levels - 1:
            environ, mixed_op = lax.optimization_barrier((environ, mixed_op))
        partner = partner_2(environ, "blk", level_idx)
        carried = jnp.dot(
            jnp.dot(couple_mat, partner, precision=highest), couple_mat.T, precision=highest
        )
        environ = 0.5 * (environ + carried)
    grams = pl.pallas_call(
        gram_kernel,
        grid=(steps,),
        in_specs=[rows_spec, whole(square)],
        out_specs=[whole(square)] * 3,
        out_shape=[jax.ShapeDtypeStruct(square, f32)] * 3,
        compiler_params=params,
        cost_estimate=pl.CostEstimate(flops=4 * work, bytes_accessed=2 * iso.size, transcendentals=0),
        name="gram",
    )(rows, mixed_op)
    top_low = environ.astype(bf16)
    packed = pl.pallas_call(
        join_kernel,
        out_shape=jax.ShapeDtypeStruct((chi + TAIL, chi), bf16),
        compiler_params=pltpu.CompilerParams(vmem_limit_bytes=8 * 1024 * 1024),
        name="join",
    )(*grams, top_low)
    packed = lax.all_gather(packed, "bond", axis=0)
    updated = pl.pallas_call(
        update_kernel,
        grid=(steps,),
        in_specs=[rows_spec, whole(square), whole(square), whole(packed.shape)],
        out_specs=iso_spec,
        out_shape=jax.ShapeDtypeStruct(iso.shape, bf16),
        scratch_shapes=[
            pltpu.VMEM((chunk, *square), bf16),
            pltpu.VMEM(square, bf16),
            pltpu.VMEM((1, chi), f32),
        ],
        compiler_params=params,
        cost_estimate=pl.CostEstimate(flops=3 * work, bytes_accessed=4 * iso.size, transcendentals=0),
        name="update",
    )(rows, mixed_op, top_low, packed)
    return (updated[None], environ[None])


def solution(mesh):
    placed = (
        P("blk", None, "bond", None),
        P("blk", None, None),
        P("blk", None, None),
        P("blk", None, None),
    )
    return jax.shard_map(
        body,
        mesh=mesh,
        in_specs=placed,
        out_specs=(P("blk", None, "bond", None), P("blk", None, None)),
        check_vma=False,
    )
```

profile of v0, /device:TPU:0, one launch (start us, length us, event | category | flops | bytes accessed | tf_op | source)
XLA Modules:
  0.0 102.0 jit_solution(5556610214579537217)
XLA Ops:
  0.6 0.0 copy-start
  0.6 1.0 %pad_maximum_fusion.edges_ref = bf16[512,256]{1,0:T(8,128)(2,1)S(1)} fusion(bf16[256,256]{1,0:T(8,128)(2,1)} %bitcast.33, bf16[256,256]{1,0:T(8,128)(2,1)} %bitcast.31), kind=kLoop, calls=%fused_computation.6 | loop fusion | flops 524288 | bytes 524288 | tf_op jit(solution)/shard_map/concatenate | solution.py:158
  1.7 0.0 copy-start.1
  1.7 19.9 %ascend.1 = (bf16[64,256,256]{2,1,0:T(8,128)(2,1)}, f32[2,256,256]{2,1,0:T(8,128)S(1)}) custom-call(bf16[256,64,256]{2,1,0:T(8,128)(2,1)} %bitcast.34, bf16[512,256]{1,0:T(8,128)(2,1)S(1)} %pad_maximum_fusion.edges_ref), custom_call_target="tpu_custom_call" | custom-call | flops 12884901888 | bytes 16777216 | tf_op jit(solution)/shard_map/ascend/pallas_call | solution.py:159
  21.6 13.5 %all_to_all.5 = f32[4,128,256]{2,1,0:T(8,128)S(1)} all-to-all(f32[4,128,256]{2,1,0:T(8,128)S(1)} %bitcast.30), channel_id=1, replica_groups=mesh['blk'=8,'bond'=4] {'bond'}, dimensions={0} | all-to-all | bytes 1048576 | tf_op jit(solution)/shard_map/all_to_all | solution.py:174
  35.1 8.6 %all_gather.9 = bf16[512,256]{1,0:T(8,128)(2,1)S(1)} all-gather(bf16[128,256]{1,0:T(8,128)(2,1)S(1)} %reduce_sum.9), channel_id=1, replica_groups=mesh['blk'=8,'bond'=4] {'bond'}, dimensions={0}, use_global_device_ids=true | all-gather | bytes 327680 | tf_op jit(solution)/shard_map/all_gather | solution.py:176
  43.7 0.1 collective-permute-start
  43.8 0.5 collective-permute-start.2
  44.4 3.3 %collective-permute-start.3 = (bf16[256,256]{1,0:T(8,128)(2,1)S(1)}, bf16[256,256]{1,0:T(8,128)(2,1)S(1)}, u32[]{:S(2)}, u32[]{:S(2)}) collective-permute-start(bf16[256,256]{1,0:T(8,128)(2,1)S(1)} %get-tuple-element.17), channel_id=1, source_target_pairs={{4,0},{8,4},{12,8},{16,12},{20,16},{24,20},{28,24},{0,28},{5,1},{9... | collective-permute-start | bytes 393224 | tf_op jit(solution)/shard_map/ppermute | solution.py:21
  47.6 0.0 collective-permute-done
  47.6 0.0 copy-done
  47.6 0.6 fusion.10
  48.2 0.6 fusion.2
  48.8 0.1 collective-permute-start.1
  48.9 1.4 %collective-permute-done.2 = bf16[256,256]{1,0:T(8,128)(2,1)S(1)} collective-permute-done((bf16[256,256]{1,0:T(8,128)(2,1)S(1)}, bf16[256,256]{1,0:T(8,128)(2,1)S(1)}, u32[]{:S(2)}, u32[]{:S(2)}) %collective-permute-start.2) | collective-permute-done | bytes 131104 | tf_op jit(solution)/shard_map/ppermute | solution.py:21
  50.3 1.2 %collective-permute-done.3 = bf16[256,256]{1,0:T(8,128)(2,1)S(1)} collective-permute-done((bf16[256,256]{1,0:T(8,128)(2,1)S(1)}, bf16[256,256]{1,0:T(8,128)(2,1)S(1)}, u32[]{:S(2)}, u32[]{:S(2)}) %collective-permute-start.3) | collective-permute-done | bytes 131104 | tf_op jit(solution)/shard_map/ppermute | solution.py:21
  51.5 0.0 copy-done.1
  51.5 0.1 add_convert_fusion.mix_ref
  51.6 5.6 %collective-permute-done.1 = f32[256,256]{1,0:T(8,128)S(1)} collective-permute-done((f32[256,256]{1,0:T(8,128)S(1)}, f32[256,256]{1,0:T(8,128)S(1)}, u32[]{:S(2)}, u32[]{:S(2)}) %collective-permute-start.1) | collective-permute-done | bytes 262176 | tf_op jit(solution)/shard_map/ppermute | solution.py:31
  57.2 0.6 fusion.7
  57.8 0.6 fusion.1
  58.4 1.2 %collective-permute-start.4 = (f32[256,256]{1,0:T(8,128)S(1)}, f32[256,256]{1,0:T(8,128)S(1)}, u32[]{:S(2)}, u32[]{:S(2)}) collective-permute-start(f32[256,256]{1,0:T(8,128)S(1)} %fusion.1), channel_id=1, source_target_pairs={{0,16},{16,0},{4,20},{20,4},{8,24},{24,8},{12,28},{28,12},{1,17},{... | collective-permute-start | bytes 786440 | tf_op jit(solution)/shard_map/ppermute | solution.py:31
  59.6 13.4 %gram.1 = (f32[256,256]{1,0:T(8,128)S(1)}, f32[256,256]{1,0:T(8,128)S(1)}, f32[256,256]{1,0:T(8,128)S(1)}) custom-call(bf16[64,256,256]{2,1,0:T(8,128)(2,1)} %get-tuple-element.9.rows_ref, bf16[256,256]{1,0:T(8,128)(2,1)S(1)} %add_convert_fusion.mix_ref), custom_call_target="tpu_custom_call" | custom-call | flops 8589934592 | bytes 8388608 | tf_op jit(solution)/shard_map/gram/pallas_call | solution.py:194
  73.0 0.0 collective-permute-done.4
  73.0 0.6 fusion.4
  73.6 1.3 %fusion.13 = (bf16[256,256]{1,0:T(8,128)(2,1)S(1)}, f32[256,256]{1,0:T(8,128)}) fusion(f32[256,256]{1,0:T(8,128)S(1)} %fusion.1, f32[256,256]{1,0:T(8,128)S(1)} %fusion.4, f32[1,256,256]{2,1,0:T(8,128)S(1)} %copy-done), kind=kOutput, calls=%fused_computation.19 | convolution fusion | flops 201523200 | bytes 1179648 | tf_op jit(solution)/shard_map/dot_general | solution.py:190
  74.9 1.3 %join.1 = bf16[272,256]{1,0:T(8,128)(2,1)S(1)} custom-call(f32[256,256]{1,0:T(8,128)S(1)} %get-tuple-element.13.self_ref, f32[256,256]{1,0:T(8,128)S(1)} %get-tuple-element.14.cross_ref, f32[256,256]{1,0:T(8,128)S(1)} %get-tuple-element.15.plain_ref, bf16[256,256]{1,0:T(8,128)(2,1)S(1)} %get-tuple-element.18.top_ref), custom_call_target="tpu_custom_call" | custom-call | tf_op jit(solution)/shard_map/join/pallas_call | solution.py:205
  76.2 10.3 %all-gather = bf16[1088,256]{1,0:T(8,128)(2,1)S(1)} all-gather(bf16[272,256]{1,0:T(8,128)(2,1)S(1)} %join.1), channel_id=2, replica_groups=mesh['blk'=8,'bond'=4] {'bond'}, dimensions={0}, use_global_device_ids=true | all-gather | bytes 696320 | tf_op jit(solution)/shard_map/all_gather | solution.py:211
  86.5 15.5 %update.1 = bf16[256,64,256]{2,1,0:T(8,128)(2,1)} custom-call(bf16[64,256,256]{2,1,0:T(8,128)(2,1)} %get-tuple-element.9.rows_ref, bf16[256,256]{1,0:T(8,128)(2,1)S(1)} %add_convert_fusion.mix_ref, bf16[256,256]{1,0:T(8,128)(2,1)S(1)} %get-tuple-element.18.top_ref, bf16[4,272,256]{2,1,0:T(8,128)(2,1)S(1)} %bitcast.29), custom_call_target="tpu_custom_call" | custom-call | flops 6442450944 | bytes 16777216 | tf_op jit(solution)/shard_map/update/pallas_call | solution.py:212
  (3 shorter events, 0.1 us)
Async XLA Ops:
  0.6 47.0 %copy-start = (f32[1,256,256]{2,1,0:T(8,128)S(1)}, f32[1,256,256]{2,1,0:T(8,128)}, u32[]{:S(2)}) copy-start(f32[1,256,256]{2,1,0:T(8,128)} %param.7) | copy-start | bytes 786436
  1.7 49.8 %copy-start.1 = (bf16[1,256,256]{2,1,0:T(8,128)(2,1)S(1)}, bf16[1,256,256]{2,1,0:T(8,128)(2,1)}, u32[]{:S(2)}) copy-start(bf16[1,256,256]{2,1,0:T(8,128)(2,1)} %param.5) | copy-start | bytes 393220
  43.7 3.9 %collective-permute-start = (f32[256,256]{1,0:T(8,128)S(1)}, f32[256,256]{1,0:T(8,128)S(1)}, u32[]{:S(2)}, u32[]{:S(2)}) collective-permute-start(f32[256,256]{1,0:T(8,128)S(1)} %convert_add_fusion), channel_id=1, source_target_pairs={{0,4},{4,0},{8,12},{12,8},{16,20},{20,16},{24,28},{28,24},{1,5},{5... | collective-permute-start | bytes 786440 | tf_op jit(solution)/shard_map/ppermute | solution.py:31
  43.8 6.5 %collective-permute-start.2 = (bf16[256,256]{1,0:T(8,128)(2,1)S(1)}, bf16[256,256]{1,0:T(8,128)(2,1)S(1)}, u32[]{:S(2)}, u32[]{:S(2)}) collective-permute-start(bf16[256,256]{1,0:T(8,128)(2,1)S(1)} %get-tuple-element.16), channel_id=1, source_target_pairs={{28,0},{0,4},{4,8},{8,12},{12,16},{16,20},{20,24},{24,28},{29,1},{... | collective-permute-start | bytes 393224 | tf_op jit(solution)/shard_map/ppermute | solution.py:21
  44.4 7.1 %collective-permute-start.3 = (bf16[256,256]{1,0:T(8,128)(2,1)S(1)}, bf16[256,256]{1,0:T(8,128)(2,1)S(1)}, u32[]{:S(2)}, u32[]{:S(2)}) collective-permute-start(bf16[256,256]{1,0:T(8,128)(2,1)S(1)} %get-tuple-element.17), channel_id=1, source_target_pairs={{4,0},{8,4},{12,8},{16,12},{20,16},{24,20},{28,24},{0,28},{5,1},{9... | collective-permute-start | bytes 393224 | tf_op jit(solution)/shard_map/ppermute | solution.py:21
  48.8 8.3 %collective-permute-start.1 = (f32[256,256]{1,0:T(8,128)S(1)}, f32[256,256]{1,0:T(8,128)S(1)}, u32[]{:S(2)}, u32[]{:S(2)}) collective-permute-start(f32[256,256]{1,0:T(8,128)S(1)} %fusion.2), channel_id=1, source_target_pairs={{0,8},{8,0},{4,12},{12,4},{16,24},{24,16},{20,28},{28,20},{1,9},{9... | collective-permute-start | bytes 786440 | tf_op jit(solution)/shard_map/ppermute | solution.py:31
  58.4 14.7 %collective-permute-start.4 = (f32[256,256]{1,0:T(8,128)S(1)}, f32[256,256]{1,0:T(8,128)S(1)}, u32[]{:S(2)}, u32[]{:S(2)}) collective-permute-start(f32[256,256]{1,0:T(8,128)S(1)} %fusion.1), channel_id=1, source_target_pairs={{0,16},{16,0},{4,20},{20,4},{8,24},{24,8},{12,28},{28,12},{1,17},{... | collective-permute-start | bytes 786440 | tf_op jit(solution)/shard_map/ppermute | solution.py:31
where the time goes:
time: 102 us
  Pallas kernels  50 us (49%)
  blocking collectives  32.4 us (32%)
  waiting for transfers between devices  8.18 us (8%)
  starting transfers between devices  5.19 us (5%)
  matrix products  4.28 us (4%)
  other arithmetic  1.15 us (1%)
    pallas_call x1, Pallas kernels, body(): pl.pallas_call(ascend_kernel, grid=(steps,), in_specs=[iso_spec, whole((2...  19.9 us
    pallas_call x1, Pallas kernels, body(): pl.pallas_call(update_kernel, grid=(steps,), in_specs=[rows_spec, whole(s...  15.5 us
    all_to_all x1, blocking collectives, body(): pieces = lax.all_to_all(pieces, 'bond', 0, 0, tiled=True)  13.5 us
    pallas_call x1, Pallas kernels, body(): pl.pallas_call(gram_kernel, grid=(steps,), in_specs=[rows_spec, whole(squ...  13.4 us
    all_gather x1, blocking collectives, body(): packed = lax.all_gather(packed, 'bond', axis=0)  10.3 us
    all_gather x1, blocking collectives, body(): lax.all_gather(piece, 'bond', axis=0, tiled=True).reshape(2, *square)  8.6 us
    ppermute x3, waiting for transfers between devices, partner_2(): return lax.ppermute(block, axis, route)  5.59 us
    ppermute x2, starting transfers between devices, shifted(): return lax.ppermute(block, axis, route)  3.8 us
  transfers between devices with their start and end apart: 5, of which 3 were waited for; matrix products, arithmetic and copies ran while one was open for 1% of the time, Pallas kernels for 13%

commit v1 on v0

v1 whole, which is shorter than its diff:
```python
import functools

import jax
import jax.numpy as jnp
from jax import lax
from jax.experimental import pallas as pl
from jax.experimental.pallas import tpu as pltpu
from jax.sharding import PartitionSpec as P

NEWTON = 2
CHUNK = 16
GROUP = 4
SLAB = 8

highest = lax.Precision.HIGHEST
f32 = jnp.float32
bf16 = jnp.bfloat16
MESH = pl.DeviceIdType.MESH


def mm(a, b):
    return jnp.dot(a, b, preferred_element_type=f32)


def exact(a, b):
    return jnp.dot(a, b, precision=highest, preferred_element_type=f32)


def exact_turned(a, b):
    return lax.dot_general(
        a, b, (((1,), (1,)), ((), ())), precision=highest, preferred_element_type=f32
    )


def diagonal(shape):
    return lax.broadcasted_iota(jnp.int32, shape, 0) == lax.broadcasted_iota(jnp.int32, shape, 1)


def flipped(index, mask):
    out = index
    bit = 1
    while bit <= mask:
        if mask & bit:
            out = out + bit * (1 - 2 * lax.rem(index // bit, 2))
        bit *= 2
    return out


def halves(value):
    high = value.astype(bf16)
    return high, (value - high.astype(f32)).astype(bf16)


def sweep_kernel(
    blk, bond, levels,
    iso_ref, left_ref, right_ref, couple_ref,
    rows_out, mix_out, top_out, env_out, gram_out, trace_out,
    stage, even, odd, total, heard, asc, around, other, mixed, envs, far, grams, packed, traces,
    in_sem, out_sem, rs_send, rs_recv, ag_send, ag_recv, nb_send, nb_recv, zero_send, zero_recv,
    mix_send, mix_recv, dir_send, dir_recv, fw_send, fw_recv, gr_send, gr_recv, tr_send, tr_recv,
):
    s = lax.axis_index("blk")
    r = lax.axis_index("bond")
    chi = left_ref.shape[0]
    chunks = stage.shape[0]
    half = chunks // 2
    piece = chi // bond
    square = (chi, chi)
    cut = (bond, piece, chi)
    after = lax.rem(s + 1, blk)
    before = lax.rem(s + blk - 1, blk)
    masks = range(1, bond)
    pending = []

    loads = [
        pltpu.make_async_copy(iso_ref.at[:, pl.ds(SLAB * c, SLAB), :], stage.at[c], in_sem.at[c])
        for c in range(chunks)
    ]
    for load in loads:
        load.start()

    barrier = pltpu.get_barrier_semaphore()
    partners = [flipped(s, 1 << level) for level in range(levels)]
    greeted = [(s, flipped(r, mask)) for mask in masks]
    greeted += [(after, r), (before, r)] + [(t, r) for t in partners]
    for device in greeted:
        pl.semaphore_signal(barrier, inc=1, device_id=device, device_id_type=MESH)

    def send(src, dst, out_flag, in_flag, device):
        copy = pltpu.make_async_remote_copy(
            src_ref=src, dst_ref=dst, send_sem=out_flag, recv_sem=in_flag,
            device_id=device, device_id_type=MESH,
        )
        copy.start()
        pending.append(copy)
        return copy

    def relayout(c, dst, i):
        dst[i] = jnp.transpose(stage[c], (1, 0, 2))

    def ascend(k, edge_ref, src, i):
        for first in range(0, SLAB, GROUP):
            mats = [src[i, first + j] for j in range(GROUP)]
            turned = jnp.concatenate(mats, axis=0).T
            both = jnp.concatenate([mm(edge_ref[...], one) for one in mats], axis=0)
            high, low = halves(both)
            total[k] += (mm(turned, high) + mm(turned, low)).reshape(cut)

    total[...] = jnp.zeros_like(total)
    grams[...] = jnp.zeros_like(grams)
    loads[0].wait()
    relayout(0, even, 0)

    def load_wait(c):
        pltpu.make_async_copy(
            iso_ref.at[:, pl.ds(0, SLAB), :], stage.at[c], in_sem.at[c]
        ).wait()

    def first_pass(i, carry):
        load_wait(2 * i + 1)
        relayout(2 * i + 1, odd, i)
        ascend(0, left_ref, even, i)

        @pl.when(i + 1 < half)
        def _():
            load_wait(2 * i + 2)

        relayout(lax.rem(2 * i + 2, chunks), even, i + 1)
        ascend(0, left_ref, odd, i)
        return carry

    lax.fori_loop(0, half, first_pass, 0)
    pl.semaphore_wait(barrier, len(greeted))

    def scatter(k):
        return [
            send(total.at[k, flipped(r, mask)], heard.at[k, mask - 1],
                 rs_send.at[k, mask - 1], rs_recv.at[k, mask - 1], (s, flipped(r, mask)))
            for mask in masks
        ]

    def gather(k):
        return [
            send(asc.at[k, r], asc.at[k, r], ag_send.at[k, mask - 1], ag_recv.at[k, mask - 1],
                 (s, flipped(r, mask)))
            for mask in masks
        ]

    def reduced(k, copies):
        for copy in copies:
            copy.wait_recv()
        own = total[k, r]
        for mask in masks:
            own = own + heard[k, mask - 1]
        asc[k, r] = own.astype(bf16)

    def arrived(copies):
        for copy in copies:
            copy.wait_recv()

    def second_pass(i, carry):
        ascend(1, right_ref, even, i)
        ascend(1, right_ref, odd, i)
        return carry

    scattered_left = scatter(0)
    early = half * 3 // 4
    lax.fori_loop(0, early, second_pass, 0)
    reduced(0, scattered_left)
    gathered_left = gather(0)
    to_before = send(asc.at[0, r], around.at[0], nb_send.at[0], nb_recv.at[0], (before, r))
    lax.fori_loop(early, half, second_pass, 0)
    scattered_right = scatter(1)

    stores = []
    for c in range(chunks):
        src = (odd if c % 2 else even).at[c // 2]
        store = pltpu.make_async_copy(src, rows_out.at[pl.ds(SLAB * c, SLAB)], out_sem.at[c])
        store.start()
        stores.append(store)

    def plain_pass(i, carry):
        for src in (even, odd):
            for first in range(0, SLAB, GROUP):
                rows = jnp.concatenate([src[i, first + j] for j in range(GROUP)], axis=0)
                grams[2] += mm(rows.T, rows)
        return carry

    lax.fori_loop(0, half, plain_pass, 0)
    arrived(gathered_left)
    zero_left = send(asc.at[0], other.at[0], zero_send.at[0], zero_recv.at[0], (partners[0], r))
    reduced(1, scattered_right)
    gathered_right = gather(1)
    to_after = send(asc.at[1, r], around.at[1], nb_send.at[1], nb_recv.at[1], (after, r))
    arrived(gathered_right)
    zero_right = send(asc.at[1], other.at[1], zero_send.at[1], zero_recv.at[1], (partners[0], r))
    envs[0] = asc[0].astype(f32) + asc[1].astype(f32)
    arrived([to_before, to_after])
    mine = left_ref[pl.ds(pl.multiple_of(r * piece, piece), piece), :].astype(f32)
    mixed[r] = (mine + around[1].astype(f32) + around[0].astype(f32)).astype(bf16)
    gathered_mix = [
        send(mixed.at[r], mixed.at[r], mix_send.at[mask - 1], mix_recv.at[mask - 1],
             (s, flipped(r, mask)))
        for mask in masks
    ]

    def climb(level, partner):
        couple = couple_ref[...]
        carried = exact_turned(exact(couple, partner.reshape(square)), couple)
        envs[level + 1] = 0.5 * (envs[level] + carried.reshape(cut))

    arrived([zero_left, zero_right])
    climb(0, other[0].astype(f32) + other[1].astype(f32))

    def gram_pass(i, carry):
        mix = mixed[...].reshape(square)
        for src in (even, odd):
            for first in range(0, SLAB, GROUP):
                mats = [src[i, first + j] for j in range(GROUP)]
                rows = jnp.concatenate(mats, axis=0)
                moved = jnp.concatenate([mm(mix, one).astype(bf16) for one in mats], axis=0)
                turned = moved.T
                grams[0] += mm(turned, moved)
                grams[1] += mm(turned, rows)
        return carry

    slots = 2 * (levels - 1)

    def gram_slot(slot):
        lax.fori_loop(slot * half // slots, (slot + 1) * half // slots, gram_pass, 0)

    opposite = bond - 1
    for level in range(1, levels):
        target = (partners[level], r)
        direct = [
            send(envs.at[level, place], far.at[level - 1, place],
                 dir_send.at[level - 1, n], dir_recv.at[level - 1, n], target)
            for n, place in enumerate((r, flipped(r, opposite)))
        ]
        if level == 1:
            arrived(gathered_mix)
        gram_slot(2 * (level - 1))
        direct[0].wait_recv()
        passed = [
            send(far.at[level - 1, r], far.at[level - 1, r],
                 fw_send.at[level - 1, mask - 1], fw_recv.at[level - 1, mask - 1],
                 (s, flipped(r, mask)))
            for mask in masks if mask != opposite
        ]
        gram_slot(2 * (level - 1) + 1)
        direct[1].wait_recv()
        arrived(passed)
        climb(level, far[level - 1])

    env = envs[levels].reshape(square)
    top = env.astype(bf16)
    wide = top.astype(f32)
    crossed = exact(grams[1] + 0.5 * exact(wide.T, grams[2]), wide)
    gram = grams[0] + crossed + crossed.T
    packed[r] = gram.astype(bf16)
    trace = jnp.sum(jnp.where(diagonal(gram.shape), gram, 0.0), keepdims=True)
    traces[r] = jnp.broadcast_to(trace, traces.shape[1:])
    gathered_gram = []
    for mask in masks:
        device = (s, flipped(r, mask))
        gathered_gram.append(send(
            packed.at[r], packed.at[r], gr_send.at[mask - 1], gr_recv.at[mask - 1], device))
        gathered_gram.append(send(
            traces.at[r], traces.at[r], tr_send.at[mask - 1], tr_recv.at[mask - 1], device))
    env_out[...] = env
    top_out[...] = top
    mix_out[...] = mixed[...].reshape(square)
    for store in stores:
        store.wait()
    arrived(gathered_gram)
    gram_out[...] = packed[...]
    trace_out[...] = traces[...]
    for copy in pending:
        copy.wait_send()


def update_kernel(
    rows_ref, mix_ref, top_ref, env_ref, gram_ref, trace_ref, out_ref, env_out,
    held_ref, rest_ref, mean_ref,
):
    @pl.when(pl.program_id(0) == 0)
    def _():
        env_out[...] = env_ref[...]
        gram = gram_ref[0].astype(f32)
        squares = trace_ref[0]
        for rank in range(1, gram_ref.shape[0]):
            gram = gram + gram_ref[rank].astype(f32)
            squares = squares + trace_ref[rank]
        scale = lax.rsqrt(squares[0:1, 0:1] + 1e-06)
        first_gram = gram * (scale * scale)
        gram = first_gram
        eye = diagonal(gram.shape).astype(f32)
        total = eye
        for newton_step in range(NEWTON):
            step = 1.5 * eye - 0.5 * gram
            total = step if newton_step == 0 else exact(total, step)
            if newton_step + 1 < NEWTON:
                gram = exact(exact(step, gram), step)
        energy = jnp.sum(first_gram * eye, keepdims=True)
        mean = jnp.sum(first_gram * total, keepdims=True) / jnp.maximum(energy, 1e-30)
        rest_ref[...] = ((total - mean * eye) * scale).astype(bf16)
        mean_ref[...] = jnp.broadcast_to(mean * scale, mean_ref.shape)

    mean = mean_ref[...]

    def step(g, carry):
        mats = [rows_ref[g * GROUP + j] for j in range(GROUP)]
        rows = jnp.concatenate(mats, axis=0)
        moved = jnp.concatenate([mm(mix_ref[...], one) for one in mats], axis=0)
        grad = moved + mm(rows, top_ref[...])
        done = (mean * grad + mm(grad.astype(bf16), rest_ref[...])).astype(bf16)
        held_ref[pl.ds(g * GROUP, GROUP)] = done.reshape(GROUP, *mix_ref.shape)
        return carry

    lax.fori_loop(0, rows_ref.shape[0] // GROUP, step, 0, unroll=2)
    out_ref[...] = jnp.transpose(held_ref[...], (1, 0, 2))


def whole(shape):
    return pl.BlockSpec(shape, lambda i: (0,) * len(shape))


def body(iso, edge_left, edge_right, coupling):
    iso = iso[0]
    chi, depth, _ = iso.shape
    blk = lax.axis_size("blk")
    bond = lax.axis_size("bond")
    levels = blk.bit_length() - 1
    square = (chi, chi)
    piece = chi // bond
    chunks = depth // SLAB
    half = chunks // 2
    work = 2 * depth * chi**3
    dma = pltpu.SemaphoreType.DMA
    vmem = pl.BlockSpec(memory_space=pltpu.VMEM)
    hbm = pl.BlockSpec(memory_space=pl.ANY)
    rows, mix, top, environ, grams, traces = pl.pallas_call(
        functools.partial(sweep_kernel, blk, bond, levels),
        in_specs=[hbm, vmem, vmem, vmem],
        out_specs=[hbm] + [vmem] * 5,
        out_shape=[
            jax.ShapeDtypeStruct((depth, *square), bf16),
            jax.ShapeDtypeStruct(square, bf16),
            jax.ShapeDtypeStruct(square, bf16),
            jax.ShapeDtypeStruct(square, f32),
            jax.ShapeDtypeStruct((bond, *square), bf16),
            jax.ShapeDtypeStruct((bond, 8, 128), f32),
        ],
        scratch_shapes=[
            pltpu.VMEM((chunks, chi, SLAB, chi), bf16),
            pltpu.VMEM((half + 1, SLAB, *square), bf16),
            pltpu.VMEM((half, SLAB, *square), bf16),
            pltpu.VMEM((2, bond, piece, chi), f32),
            pltpu.VMEM((2, bond - 1, piece, chi), f32),
            pltpu.VMEM((2, bond, piece, chi), bf16),
            pltpu.VMEM((2, piece, chi), bf16),
            pltpu.VMEM((2, bond, piece, chi), bf16),
            pltpu.VMEM((bond, piece, chi), bf16),
            pltpu.VMEM((levels + 1, bond, piece, chi), f32),
            pltpu.VMEM((levels - 1, bond, piece, chi), f32),
            pltpu.VMEM((3, *square), f32),
            pltpu.VMEM((bond, *square), bf16),
            pltpu.VMEM((bond, 8, 128), f32),
            dma((chunks,)), dma((chunks,)),
            dma((2, bond - 1)), dma((2, bond - 1)),
            dma((2, bond - 1)), dma((2, bond - 1)),
            dma((2,)), dma((2,)), dma((2,)), dma((2,)),
            dma((bond - 1,)), dma((bond - 1,)),
            dma((levels - 1, 2)), dma((levels - 1, 2)),
            dma((levels - 1, bond - 1)), dma((levels - 1, bond - 1)),
            dma((bond - 1,)), dma((bond - 1,)),
            dma((bond - 1,)), dma((bond - 1,)),
        ],
        compiler_params=pltpu.CompilerParams(
            vmem_limit_bytes=48 * 1024 * 1024, collective_id=0, has_side_effects=True
        ),
        cost_estimate=pl.CostEstimate(flops=10 * work, bytes_accessed=4 * iso.size, transcendentals=0),
        name="sweep",
    )(iso, edge_left[0], edge_right[0], coupling[0])
    chunk = CHUNK if depth % CHUNK == 0 else depth
    iso_spec = pl.BlockSpec((chi, chunk, chi), lambda i: (0, i, 0))
    rows_spec = pl.BlockSpec((chunk, chi, chi), lambda i: (i, 0, 0))
    updated, environ = pl.pallas_call(
        update_kernel,
        grid=(depth // chunk,),
        in_specs=[rows_spec] + [whole(square)] * 3 + [whole(grams.shape), whole(traces.shape)],
        out_specs=[iso_spec, whole(square)],
        out_shape=[
            jax.ShapeDtypeStruct(iso.shape, bf16),
            jax.ShapeDtypeStruct(square, f32),
        ],
        scratch_shapes=[
            pltpu.VMEM((chunk, *square), bf16),
            pltpu.VMEM(square, bf16),
            pltpu.VMEM((1, chi), f32),
        ],
        compiler_params=pltpu.CompilerParams(
            dimension_semantics=("arbitrary",), vmem_limit_bytes=48 * 1024 * 1024
        ),
        cost_estimate=pl.CostEstimate(flops=3 * work, bytes_accessed=4 * iso.size, transcendentals=0),
        name="update",
    )(rows, mix, top, environ, grams, traces)
    return (updated[None], environ[None])


def solution(mesh):
    placed = (
        P("blk", None, "bond", None),
        P("blk", None, None),
        P("blk", None, None),
        P("blk", None, None),
    )
    return jax.shard_map(
        body,
        mesh=mesh,
        in_specs=placed,
        out_specs=(P("blk", None, "bond", None), P("blk", None, None)),
        check_vma=False,
    )
```

time: 102 us -> 87.3 us (0.86)
  Pallas kernels: 50 us -> 83.7 us
  blocking collectives: 32.4 us -> 0 us
  waiting for transfers between devices: 8.18 us -> 0 us
  starting transfers between devices: 5.19 us -> 0 us
  matrix products: 4.28 us -> 0 us
  local copies, waits for them, and re-layouts: 0.04 us -> 2.75 us
  other arithmetic: 1.15 us -> 0 us
    pallas_call x4 -> x2, Pallas kernels: 50 us -> 83.7 us  [the longest x1 67.9 us: body(): pl.pallas_call(functools.partial(sweep_kernel, blk, bond, levels), in_spe...]
    all_gather x2 -> x0, blocking collectives: 18.9 us -> none  [the longest x1 10.3 us: body(): packed = lax.all_gather(packed, 'bond', axis=0)]
    all_to_all x1 -> x0, blocking collectives: 13.5 us -> none  [body(): pieces = lax.all_to_all(pieces, 'bond', 0, 0, tiled=True)]
    ppermute x5 -> x0, waiting for transfers between devices: 8.18 us -> none  [the longest x3 5.59 us: partner_2(): return lax.ppermute(block, axis, route)]
    ppermute x5 -> x0, starting transfers between devices: 5.19 us -> none  [the longest x2 3.8 us: shifted(): return lax.ppermute(block, axis, route)]
    dot_general x6 -> x0, matrix products: 4.28 us -> none  [the longest x3 2.5 us: body(): jnp.dot(jnp.dot(couple_mat, partner, precision=highest), couple_mat.T, pr...]
    unnamed x4 -> x6, local copies, waits for them, and re-layouts: 0.02 us -> 2.75 us
    concatenate x1 -> x0, other arithmetic: 1.03 us -> none  [body(): edges = jnp.concatenate([edge_left[0], edge_right[0]], axis=0)]
  transfers between devices with their start and end apart: 5 -> 0, of which waited for: 3 -> 0; matrix products, arithmetic and copies ran while one was open for 1% -> 0% of each run, Pallas kernels for 13% -> 0%
where the time goes in v1:
time: 87.3 us; the launch traced here: 87.1 us
  Pallas kernels  83.7 us (96%)
  local copies, waits for them, and re-layouts  2.75 us (3%)
    pallas_call x1, Pallas kernels, body(): pl.pallas_call(functools.partial(sweep_kernel, blk, bond, levels), in_spe...  67.9 us
    pallas_call x1, Pallas kernels, body(): pl.pallas_call(update_kernel, grid=(depth // chunk,), in_specs=[rows_spec...  15.8 us
    unnamed x6, local copies, waits for them, and re-layouts  2.75 us

profile of v1, /device:TPU:0, one launch (start us, length us, event | category | flops | bytes accessed | tf_op | source)
XLA Modules:
  0.0 87.1 jit_solution(16392274333991237760)
XLA Ops:
  0.6 0.0 copy-start
  0.6 0.9 %copy-done = f32[1,256,256]{2,1,0:T(8,128)S(1)} copy-done((f32[1,256,256]{2,1,0:T(8,128)S(1)}, f32[1,256,256]{2,1,0:T(8,128)}, u32[]{:S(2)}) %copy-start) | copy-done | bytes 262168
  1.6 0.0 copy-start.1
  1.6 0.9 %copy-done.1 = bf16[1,256,256]{2,1,0:T(8,128)(2,1)S(1)} copy-done((bf16[1,256,256]{2,1,0:T(8,128)(2,1)S(1)}, bf16[1,256,256]{2,1,0:T(8,128)(2,1)}, u32[]{:S(2)}) %copy-start.1) | copy-done | bytes 131096
  2.5 0.0 copy-start.2
  2.5 0.9 %copy-done.2 = bf16[1,256,256]{2,1,0:T(8,128)(2,1)S(1)} copy-done((bf16[1,256,256]{2,1,0:T(8,128)(2,1)S(1)}, bf16[1,256,256]{2,1,0:T(8,128)(2,1)}, u32[]{:S(2)}) %copy-start.2) | copy-done | bytes 131096
  3.4 67.9 %sweep.1 = (bf16[64,256,256]{2,1,0:T(8,128)(2,1)}, bf16[256,256]{1,0:T(8,128)(2,1)S(1)}, bf16[256,256]{1,0:T(8,128)(2,1)S(1)}, f32[256,256]{1,0:T(8,128)S(1)}, b...) custom-call(bf16[256,64,256]{2,1,0:T(8,128)(2,1)} %bitcast.9, bf16[256,256]{1,0:T(8,128)(2,1)S(1)} %bitcast.7, ...), custom_call_target="tpu_custom_call" | custom-call | flops 21474836480 | bytes 16777216 | tf_op jit(solution)/shard_map/sweep/pallas_call | solution.py:342
  71.2 15.8 %update.1 = (bf16[256,64,256]{2,1,0:T(8,128)(2,1)}, f32[256,256]{1,0:T(8,128)}) custom-call(bf16[64,256,256]{2,1,0:T(8,128)(2,1)} %get-tuple-element.10.rows_ref, bf16[256,256]{1,0:T(8,128)(2,1)S(1)} %get-tuple-element.11.mix_ref, bf16[256,256]{1,0:T(8,128)(2,1)S(1)} %get-tuple-element.12.top_ref, f32[256,256]{1,0:T(8,128)S(1)} %get-tuple-element.13.env_ref, ...), custom_call_target="tpu_custom_call" | custom-call | flops 6442450944 | bytes 16777216 | tf_op jit(solution)/shard_map/update/pallas_call | solution.py:388
Async XLA Ops:
  0.6 1.0 %copy-start = (f32[1,256,256]{2,1,0:T(8,128)S(1)}, f32[1,256,256]{2,1,0:T(8,128)}, u32[]{:S(2)}) copy-start(f32[1,256,256]{2,1,0:T(8,128)} %param.7) | copy-start | bytes 786436
  1.6 0.9 %copy-start.1 = (bf16[1,256,256]{2,1,0:T(8,128)(2,1)S(1)}, bf16[1,256,256]{2,1,0:T(8,128)(2,1)}, u32[]{:S(2)}) copy-start(bf16[1,256,256]{2,1,0:T(8,128)(2,1)} %param.5) | copy-start | bytes 393220
  2.5 0.9 %copy-start.2 = (bf16[1,256,256]{2,1,0:T(8,128)(2,1)S(1)}, bf16[1,256,256]{2,1,0:T(8,128)(2,1)}, u32[]{:S(2)}) copy-start(bf16[1,256,256]{2,1,0:T(8,128)(2,1)} %param.6) | copy-start | bytes 393220

commit v2 on v1

v2 whole, which is shorter than its diff:
```python
import functools

import jax
import jax.numpy as jnp
from jax import lax
from jax.experimental import pallas as pl
from jax.experimental.pallas import tpu as pltpu
from jax.sharding import PartitionSpec as P

GROUP = 4
SLAB = 8
SWEEP_VMEM = 61 * 1024 * 1024
UPDATE_VMEM = 61 * 1024 * 1024

highest = lax.Precision.HIGHEST
f32 = jnp.float32
bf16 = jnp.bfloat16
MESH = pl.DeviceIdType.MESH


def mm(a, b):
    return jnp.dot(a, b, preferred_element_type=f32)


def exact(a, b):
    return jnp.dot(a, b, precision=highest, preferred_element_type=f32)


def exact_turned(a, b):
    return lax.dot_general(
        a, b, (((1,), (1,)), ((), ())), precision=highest, preferred_element_type=f32
    )


def diagonal(shape):
    return lax.broadcasted_iota(jnp.int32, shape, 0) == lax.broadcasted_iota(jnp.int32, shape, 1)


def flipped(index, mask):
    out = index
    bit = 1
    while bit <= mask:
        if mask & bit:
            out = out + bit * (1 - 2 * lax.rem(index // bit, 2))
        bit *= 2
    return out


def halves(value):
    high = value.astype(bf16)
    return high, (value - high.astype(f32)).astype(bf16)


def sweep_kernel(
    blk, bond, levels,
    iso_ref, left_in, right_in, couple_in,
    grad_out, env_out, gram_out, trace_out,
    left_ref, right_ref, couple_ref, grad, stage, even, odd, turn_even, turn_odd,
    high_even, low_even, high_odd, low_odd, total, heard, asc, around, other, mixed, envs, far, grams, packed, traces,
    in_sem, small_sem, grad_sem, tail_sem, rs_send, rs_recv, ag_send, ag_recv, nb_send, nb_recv, zero_send, zero_recv,
    mix_send, mix_recv, dir_send, dir_recv, fw_send, fw_recv, gr_send, gr_recv, tr_send, tr_recv,
):
    s = lax.axis_index("blk")
    r = lax.axis_index("bond")
    chi = left_ref.shape[0]
    chunks = iso_ref.shape[1] // SLAB
    slots_in = stage.shape[0]
    half = chunks // 2
    piece = chi // bond
    square = (chi, chi)
    cut = (bond, piece, chi)
    after = lax.rem(s + 1, blk)
    before = lax.rem(s + blk - 1, blk)
    masks = range(1, bond)
    pending = []

    def load(c):
        slot = lax.rem(c, slots_in)
        first = c * SLAB if isinstance(c, int) else pl.multiple_of(c * SLAB, SLAB)
        return pltpu.make_async_copy(
            iso_ref.at[:, pl.ds(first, SLAB), :], stage.at[slot], in_sem.at[slot]
        )

    small = [
        pltpu.make_async_copy(src, dst, small_sem.at[n])
        for n, (src, dst) in enumerate(
            ((left_in, left_ref), (right_in, right_ref), (couple_in, couple_ref))
        )
    ]
    load(0).start()
    for copy in small:
        copy.start()
    load(1).start()

    barrier = pltpu.get_barrier_semaphore()
    partners = [flipped(s, 1 << level) for level in range(levels)]
    greeted = [(s, flipped(r, mask)) for mask in masks]
    greeted += [(after, r), (before, r)] + [(t, r) for t in partners]
    for device in greeted:
        pl.semaphore_signal(barrier, inc=1, device_id=device, device_id_type=MESH)

    def send(src, dst, out_flag, in_flag, device):
        copy = pltpu.make_async_remote_copy(
            src_ref=src, dst_ref=dst, send_sem=out_flag, recv_sem=in_flag,
            device_id=device, device_id_type=MESH,
        )
        copy.start()
        pending.append(copy)
        return copy

    def relayout(c, dst, i):
        dst[i] = jnp.transpose(stage[lax.rem(c, slots_in)], (1, 0, 2))

    def spread(edge_ref, src, i, turn, high, low):
        for j in range(SLAB):
            one = src[i, j]
            place = slice(j * chi, (j + 1) * chi)
            high[place, :], low[place, :] = halves(mm(edge_ref[...], one))
            if turn is not None:
                turn[i, :, place] = one.T

    def collect(k, turn, i, high, low):
        turned = turn[i]
        total[k] += (mm(turned, high[...]) + mm(turned, low[...])).reshape(cut)

    even_parts = (high_even, low_even)
    odd_parts = (high_odd, low_odd)
    total[...] = jnp.zeros_like(total)
    grams[...] = jnp.zeros_like(grams)
    load(0).wait()
    for c in range(2, min(4, chunks)):
        load(c).start()
    for copy in small:
        copy.wait()
    relayout(0, even, 0)
    spread(left_ref, even, 0, turn_even, *even_parts)
    load(1).wait()
    relayout(1, odd, 0)

    def first_pass(i, carry):
        for ahead in (2, 3):
            @pl.when(2 * i + ahead < chunks)
            def _():
                load(2 * i + ahead).wait()

            @pl.when(2 * i + ahead + 2 < chunks)
            def _():
                load(2 * i + ahead + 2).start()

        collect(0, turn_even, i, *even_parts)
        spread(left_ref, odd, i, turn_odd, *odd_parts)
        relayout(2 * i + 2, even, i + 1)
        collect(0, turn_odd, i, *odd_parts)
        spread(left_ref, even, i + 1, turn_even, *even_parts)
        relayout(2 * i + 3, odd, i + 1)
        return carry

    with jax.named_scope('first'):
        lax.fori_loop(0, half, first_pass, 0)
    pl.semaphore_wait(barrier, len(greeted))

    def scatter(k):
        return [
            send(total.at[k, flipped(r, mask)], heard.at[k, mask - 1],
                 rs_send.at[k, mask - 1], rs_recv.at[k, mask - 1], (s, flipped(r, mask)))
            for mask in masks
        ]

    def gather(k):
        return [
            send(asc.at[k, r], asc.at[k, r], ag_send.at[k, mask - 1], ag_recv.at[k, mask - 1],
                 (s, flipped(r, mask)))
            for mask in masks
        ]

    def reduced(k, copies):
        for copy in copies:
            copy.wait_recv()
        own = total[k, r]
        for mask in masks:
            own = own + heard[k, mask - 1]
        asc[k, r] = own.astype(bf16)

    def arrived(copies):
        for copy in copies:
            copy.wait_recv()

    def second_pass(i, carry):
        collect(1, turn_even, i, *even_parts)
        spread(right_ref, odd, i, None, *odd_parts)
        collect(1, turn_odd, i, *odd_parts)
        spread(right_ref, even, i + 1, None, *even_parts)
        return carry

    scattered_left = scatter(0)
    spread(right_ref, even, 0, None, *even_parts)
    early = half * 3 // 4
    with jax.named_scope('second_a'):
        lax.fori_loop(0, early, second_pass, 0)
    with jax.named_scope('w_rs0'):
        reduced(0, scattered_left)
    gathered_left = gather(0)
    to_before = send(asc.at[0, r], around.at[0], nb_send.at[0], nb_recv.at[0], (before, r))
    with jax.named_scope('second_b'):
        lax.fori_loop(early, half, second_pass, 0)
    scattered_right = scatter(1)

    def plain_pass(i, carry):
        for src, turn in ((even, turn_even), (odd, turn_odd)):
            grams[2] += mm(turn[i], src[i].reshape(SLAB * chi, chi))
        return carry

    plain_early = half // 2
    with jax.named_scope('plain'):
        lax.fori_loop(0, plain_early, plain_pass, 0)
    with jax.named_scope('w_ag0'):
        arrived(gathered_left)
    zero_left = send(asc.at[0], other.at[0], zero_send.at[0], zero_recv.at[0], (partners[0], r))
    with jax.named_scope('w_rs1'):
        reduced(1, scattered_right)
    gathered_right = gather(1)
    to_after = send(asc.at[1, r], around.at[1], nb_send.at[1], nb_recv.at[1], (after, r))
    with jax.named_scope('w_ag1'):
        arrived(gathered_right)
    zero_right = send(asc.at[1], other.at[1], zero_send.at[1], zero_recv.at[1], (partners[0], r))
    envs[0] = asc[0].astype(f32) + asc[1].astype(f32)
    def climb(level, partner):
        couple = couple_ref[...]
        carried = exact_turned(exact(couple, partner.reshape(square)), couple)
        envs[level + 1] = 0.5 * (envs[level] + carried.reshape(cut))

    with jax.named_scope('w_zero'):
        arrived([zero_left, zero_right])
    with jax.named_scope('climb0'):
        climb(0, other[0].astype(f32) + other[1].astype(f32))
    opposite = bond - 1

    def send_direct(level):
        return [
            send(envs.at[level, place], far.at[level - 1, place],
                 dir_send.at[level - 1, n], dir_recv.at[level - 1, n], (partners[level], r))
            for n, place in enumerate((r, flipped(r, opposite)))
        ]

    direct = send_direct(1)
    with jax.named_scope('w_nb'):
        arrived([to_before, to_after])
    mine = left_ref[pl.ds(pl.multiple_of(r * piece, piece), piece), :].astype(f32)
    mixed[r] = (mine + around[1].astype(f32) + around[0].astype(f32)).astype(bf16)
    gathered_mix = [
        send(mixed.at[r], mixed.at[r], mix_send.at[mask - 1], mix_recv.at[mask - 1],
             (s, flipped(r, mask)))
        for mask in masks
    ]

    def gram_pass(i, carry):
        mix = mixed[...].reshape(square)
        for src in (even, odd):
            for first in range(0, SLAB, GROUP):
                mats = [src[i, first + j] for j in range(GROUP)]
                rows = jnp.concatenate(mats, axis=0)
                moved = jnp.concatenate([mm(mix, one).astype(bf16) for one in mats], axis=0)
                turned = moved.T
                grams[0] += mm(turned, moved)
                grams[1] += mm(turned, rows)
        return carry

    shares = 2 * (levels - 1) - 1

    def gram_share(n):
        lax.fori_loop(n * half // shares, (n + 1) * half // shares, gram_pass, 0)

    for level in range(1, levels):
        if level == 1:
            with jax.named_scope('plain_late'):
                lax.fori_loop(plain_early, half, plain_pass, 0)
        else:
            direct = send_direct(level)
            with jax.named_scope('slot_a'):
                gram_share(2 * level - 3)
        with jax.named_scope('w_dir'):
            direct[0].wait_recv()
        passed = [
            send(far.at[level - 1, r], far.at[level - 1, r],
                 fw_send.at[level - 1, mask - 1], fw_recv.at[level - 1, mask - 1],
                 (s, flipped(r, mask)))
            for mask in masks if mask != opposite
        ]
        if level == 1:
            with jax.named_scope('w_mix'):
                arrived(gathered_mix)
        with jax.named_scope('slot_b'):
            gram_share(2 * level - 2)
        with jax.named_scope('w_dir1'):
            direct[1].wait_recv()
        with jax.named_scope('w_fw'):
            arrived(passed)
        with jax.named_scope('climb'):
            climb(level, far[level - 1])

    env = envs[levels].reshape(square)
    top = env.astype(bf16)
    wide = top.astype(f32)
    crossed = exact(grams[1] + 0.5 * exact(wide.T, grams[2]), wide)
    gram = grams[0] + crossed + crossed.T
    low = chi // 2
    packed[r] = jnp.concatenate([gram[:low], gram[low:, low:]], axis=1).astype(bf16)
    trace = jnp.sum(jnp.where(diagonal(gram.shape), gram, 0.0), keepdims=True)
    traces[r] = jnp.broadcast_to(trace, traces.shape[1:])
    gathered_gram = []
    for mask in masks:
        device = (s, flipped(r, mask))
        gathered_gram.append(send(
            packed.at[r], packed.at[r], gr_send.at[mask - 1], gr_recv.at[mask - 1], device))
        gathered_gram.append(send(
            traces.at[r], traces.at[r], tr_send.at[mask - 1], tr_recv.at[mask - 1], device))
    tails = [pltpu.make_async_copy(envs.at[levels], env_out, tail_sem.at[0])]
    tails[0].start()

    def grad_pass(i, carry):
        mix = mixed[...].reshape(square)
        for n, src in enumerate((even, odd)):
            for first in range(0, SLAB, GROUP):
                mats = [src[i, first + j] for j in range(GROUP)]
                rows = jnp.concatenate(mats, axis=0)
                moved = jnp.concatenate([mm(mix, one) for one in mats], axis=0)
                grad[2 * i + n, first:first + GROUP] = (moved + mm(rows, top)).reshape(GROUP, *square)
            pltpu.make_async_copy(
                grad.at[2 * i + n], grad_out.at[2 * i + n], grad_sem.at[2 * i + n]
            ).start()
        return carry

    with jax.named_scope('grad'):
        lax.fori_loop(0, half, grad_pass, 0)
    with jax.named_scope('w_gram'):
        arrived(gathered_gram)
    for n, (src, dst) in enumerate(((packed, gram_out), (traces, trace_out))):
        tails.append(pltpu.make_async_copy(src, dst, tail_sem.at[n + 1]))
        tails[-1].start()
    for copy in tails:
        copy.wait()
    for c in range(chunks):
        pltpu.make_async_copy(grad.at[c], grad_out.at[c], grad_sem.at[c]).wait()
    for copy in pending:
        copy.wait_send()


def update_kernel(
    grad_ref, env_ref, gram_ref, trace_ref, out_ref, env_out,
    grads, env, grams, traces, held, in_sem, out_sem, tail_sem,
):
    def load(c):
        return pltpu.make_async_copy(grad_ref.at[c], grads.at[c], in_sem.at[c])

    gram_copy = pltpu.make_async_copy(gram_ref, grams, tail_sem.at[0])
    trace_copy = pltpu.make_async_copy(trace_ref, traces, tail_sem.at[1])
    env_in = pltpu.make_async_copy(env_ref, env, tail_sem.at[2])
    env_back = pltpu.make_async_copy(env, env_out, tail_sem.at[3])
    gram_copy.start()
    trace_copy.start()
    for c in range(grads.shape[0]):
        load(c).start()
    env_in.start()
    chi = out_ref.shape[0]
    low = chi // 2
    gram_copy.wait()
    trace_copy.wait()
    packed = grams[0].astype(f32)
    squares = traces[0]
    for rank in range(1, grams.shape[0]):
        packed = packed + grams[rank].astype(f32)
        squares = squares + traces[rank]
    scale = lax.rsqrt(squares[0:1, 0:1] + 1e-06)
    under = jnp.concatenate([packed[:, low:chi].T, packed[:, chi:]], axis=1)
    gram = jnp.concatenate([packed[:, :chi], under], axis=0) * (scale * scale)
    eye = diagonal(gram.shape).astype(f32)
    twice = exact(gram, gram)
    bend = 1.6875 * eye - 0.5625 * gram + 0.0625 * twice
    total = 2.25 * eye - 2.4375 * gram + exact(twice, bend)
    energy = jnp.sum(gram * eye, keepdims=True)
    mean = jnp.sum(gram * total, keepdims=True) / jnp.maximum(energy, 1e-30)
    rest = ((total - mean * eye) * scale).astype(bf16)
    mean = mean * scale

    def finish(c, carry):
        load(c).wait()
        grad = grads[c].reshape(SLAB * chi, chi)
        done = (mean * grad + mm(grad.astype(bf16), rest)).astype(bf16)
        held[c] = jnp.transpose(done.reshape(SLAB, chi, chi), (1, 0, 2))
        pltpu.make_async_copy(
            held.at[c], out_ref.at[:, pl.ds(pl.multiple_of(c * SLAB, SLAB), SLAB), :], out_sem.at[c]
        ).start()
        return carry

    lax.fori_loop(0, held.shape[0], finish, 0)
    env_in.wait()
    env_back.start()
    for c in range(held.shape[0]):
        pltpu.make_async_copy(
            held.at[c], out_ref.at[:, pl.ds(c * SLAB, SLAB), :], out_sem.at[c]
        ).wait()
    env_back.wait()


def body(iso, edge_left, edge_right, coupling):
    iso = iso[0]
    chi, depth, _ = iso.shape
    blk = lax.axis_size("blk")
    bond = lax.axis_size("bond")
    levels = blk.bit_length() - 1
    square = (chi, chi)
    piece = chi // bond
    chunks = depth // SLAB
    half = chunks // 2
    work = 2 * depth * chi**3
    dma = pltpu.SemaphoreType.DMA
    hbm = pl.BlockSpec(memory_space=pltpu.HBM)
    grad, environ, grams, traces = pl.pallas_call(
        functools.partial(sweep_kernel, blk, bond, levels),
        in_specs=[hbm] * 4,
        out_specs=[hbm] * 4,
        out_shape=[
            jax.ShapeDtypeStruct((chunks, SLAB, *square), f32),
            jax.ShapeDtypeStruct((bond, piece, chi), f32),
            jax.ShapeDtypeStruct((bond, chi // 2, chi + chi // 2), bf16),
            jax.ShapeDtypeStruct((bond, 8, 128), f32),
        ],
        scratch_shapes=[
            pltpu.VMEM(square, bf16),
            pltpu.VMEM(square, bf16),
            pltpu.VMEM(square, f32),
            pltpu.VMEM((chunks, SLAB, *square), f32),
            pltpu.VMEM((min(4, chunks), chi, SLAB, chi), bf16),
            pltpu.VMEM((half + 1, SLAB, *square), bf16),
            pltpu.VMEM((half + 1, SLAB, *square), bf16),
            pltpu.VMEM((half + 1, chi, SLAB * chi), bf16),
            pltpu.VMEM((half + 1, chi, SLAB * chi), bf16),
            pltpu.VMEM((SLAB * chi, chi), bf16),
            pltpu.VMEM((SLAB * chi, chi), bf16),
            pltpu.VMEM((SLAB * chi, chi), bf16),
            pltpu.VMEM((SLAB * chi, chi), bf16),
            pltpu.VMEM((2, bond, piece, chi), f32),
            pltpu.VMEM((2, bond - 1, piece, chi), f32),
            pltpu.VMEM((2, bond, piece, chi), bf16),
            pltpu.VMEM((2, piece, chi), bf16),
            pltpu.VMEM((2, bond, piece, chi), bf16),
            pltpu.VMEM((bond, piece, chi), bf16),
            pltpu.VMEM((levels + 1, bond, piece, chi), f32),
            pltpu.VMEM((levels - 1, bond, piece, chi), f32),
            pltpu.VMEM((3, *square), f32),
            pltpu.VMEM((bond, chi // 2, chi + chi // 2), bf16),
            pltpu.VMEM((bond, 8, 128), f32),
            dma((min(4, chunks),)), dma((3,)), dma((chunks,)), dma((3,)),
            dma((2, bond - 1)), dma((2, bond - 1)),
            dma((2, bond - 1)), dma((2, bond - 1)),
            dma((2,)), dma((2,)), dma((2,)), dma((2,)),
            dma((bond - 1,)), dma((bond - 1,)),
            dma((levels - 1, 2)), dma((levels - 1, 2)),
            dma((levels - 1, bond - 1)), dma((levels - 1, bond - 1)),
            dma((bond - 1,)), dma((bond - 1,)),
            dma((bond - 1,)), dma((bond - 1,)),
        ],
        compiler_params=pltpu.CompilerParams(
            vmem_limit_bytes=SWEEP_VMEM, collective_id=0, has_side_effects=True
        ),
        cost_estimate=pl.CostEstimate(flops=10 * work, bytes_accessed=4 * iso.size, transcendentals=0),
        name="sweep",
    )(iso, edge_left[0], edge_right[0], coupling[0])
    updated, environ = pl.pallas_call(
        update_kernel,
        in_specs=[hbm] * 4,
        out_specs=[hbm] * 2,
        out_shape=[
            jax.ShapeDtypeStruct(iso.shape, bf16),
            jax.ShapeDtypeStruct((bond, piece, chi), f32),
        ],
        scratch_shapes=[
            pltpu.VMEM((chunks, SLAB, *square), f32),
            pltpu.VMEM((bond, piece, chi), f32),
            pltpu.VMEM((bond, chi // 2, chi + chi // 2), bf16),
            pltpu.VMEM((bond, 8, 128), f32),
            pltpu.VMEM((chunks, chi, SLAB, chi), bf16),
            dma((chunks,)), dma((chunks,)), dma((4,)),
        ],
        compiler_params=pltpu.CompilerParams(vmem_limit_bytes=UPDATE_VMEM),
        cost_estimate=pl.CostEstimate(flops=work, bytes_accessed=4 * iso.size, transcendentals=0),
        name="update",
    )(grad, environ, grams, traces)
    return (updated[None], environ.reshape(1, chi, chi))


def solution(mesh):
    placed = (
        P("blk", None, "bond", None),
        P("blk", None, None),
        P("blk", None, None),
        P("blk", None, None),
    )
    return jax.shard_map(
        body,
        mesh=mesh,
        in_specs=placed,
        out_specs=(P("blk", None, "bond", None), P("blk", None, None)),
        check_vma=False,
    )
```

time: 87.3 us -> 77.7 us (0.89)
  Pallas kernels: 83.7 us -> 76.7 us
  local copies, waits for them, and re-layouts: 2.75 us -> 0 us
    pallas_call x1, Pallas kernels: 67.9 us -> 64.2 us  [body(): pl.pallas_call(functools.partial(sweep_kernel, blk, bond, levels), in_spe...]
    pallas_call x1, Pallas kernels: 15.8 us -> 12.5 us  [body(): pl.pallas_call(update_kernel, in_specs=[hbm] * 4, out_specs=[hbm] * 2, ou...]
    unnamed x6 -> x0, local copies, waits for them, and re-layouts: 2.75 us -> none
where the time goes in v2:
time: 77.7 us; the launch traced here: 77.5 us
  Pallas kernels  76.7 us (99%)
  between operations  0.8 us (1%)
    pallas_call x1, Pallas kernels, body(): pl.pallas_call(functools.partial(sweep_kernel, blk, bond, levels), in_spe...  64.2 us
    pallas_call x1, Pallas kernels, body(): pl.pallas_call(update_kernel, in_specs=[hbm] * 4, out_specs=[hbm] * 2, ou...  12.5 us

profile of v2, /device:TPU:0, one launch (start us, length us, event | category | flops | bytes accessed | tf_op | source)
XLA Modules:
  0.0 77.5 jit_solution(2674909630219776764)
XLA Ops:
  0.6 64.2 %sweep.1 = (f32[8,8,256,256]{3,2,1,0:T(8,128)}, f32[4,64,256]{2,1,0:T(8,128)}, bf16[4,128,384]{2,1,0:T(8,128)(2,1)}, f32[4,8,128]{2,1,0:T(8,128)}) custom-call(bf16[256,64,256]{2,1,0:T(8,128)(2,1)} %bitcast.6, bf16[256,256]{1,0:T(8,128)(2,1)} %bitcast.10, bf16[256,256]{1,0:T(8,128)(2,1)} %bitcast.11, f32[256,256]{1,0:T(8,128)} %bitcast.8), custom_call_target="tpu_custom_call" | custom-call | flops 21474836480 | bytes 16777216 | tf_op jit(solution)/shard_map/sweep/pallas_call | solution.py:418
  64.9 12.5 %update.1 = (bf16[256,64,256]{2,1,0:T(8,128)(2,1)}, f32[4,64,256]{2,1,0:T(8,128)}) custom-call(f32[8,8,256,256]{3,2,1,0:T(8,128)} %get-tuple-element.8.grad_ref, f32[4,64,256]{2,1,0:T(8,128)} %get-tuple-element.9.env_ref, bf16[4,128,384]{2,1,0:T(8,128)(2,1)} %get-tuple-element.10.gram_ref, f32[4,8,128]{2,1,0:T(8,128)} %get-tuple-element.11.trace_ref), custom_call_target="tpu_custom_call" | custom-call | flops 2147483648 | bytes 16777216 | tf_op jit(solution)/shard_map/update/pallas_call | solution.py:469

commit v3 on v2

--- a/solution.py
+++ b/solution.py
@@ -9,10 +9,9 @@
 
 GROUP = 4
 SLAB = 8
-SWEEP_VMEM = 61 * 1024 * 1024
-UPDATE_VMEM = 61 * 1024 * 1024
-
-highest = lax.Precision.HIGHEST
+SWEEP_VMEM = 40 * 1024 * 1024
+UPDATE_VMEM = 20 * 1024 * 1024
+
 f32 = jnp.float32
 bf16 = jnp.bfloat16
 MESH = pl.DeviceIdType.MESH
@@ -22,14 +21,13 @@
     return jnp.dot(a, b, preferred_element_type=f32)
 
 
-def exact(a, b):
-    return jnp.dot(a, b, precision=highest, preferred_element_type=f32)
-
-
-def exact_turned(a, b):
-    return lax.dot_general(
-        a, b, (((1,), (1,)), ((), ())), precision=highest, preferred_element_type=f32
-    )
+def turned_mm(a, b):
+    return lax.dot_general(a, b, (((1,), (1,)), ((), ())), preferred_element_type=f32)
+
+
+def product(a, b, times=mm):
+    (ah, al), (bh, bl) = a, b
+    return times(ah, bh) + (times(ah, bl) + times(al, bh))
 
 
 def diagonal(shape):
@@ -55,9 +53,9 @@
     blk, bond, levels,
     iso_ref, left_in, right_in, couple_in,
     grad_out, env_out, gram_out, trace_out,
-    left_ref, right_ref, couple_ref, grad, stage, even, odd, turn_even, turn_odd,
+    left_ref, right_ref, couple_ref, couple_high, couple_low, stage, even, odd, turn_even, turn_odd,
     high_even, low_even, high_odd, low_odd, total, heard, asc, around, other, mixed, envs, far, grams, packed, traces,
-    in_sem, small_sem, grad_sem, tail_sem, rs_send, rs_recv, ag_send, ag_recv, nb_send, nb_recv, zero_send, zero_recv,
+    in_sem, small_sem, rs_send, rs_recv, ag_send, ag_recv, nb_send, nb_recv, zero_send, zero_recv,
     mix_send, mix_recv, dir_send, dir_recv, fw_send, fw_recv, gr_send, gr_recv, tr_send, tr_recv,
 ):
     s = lax.axis_index("blk")
@@ -132,6 +130,7 @@
         load(c).start()
     for copy in small:
         copy.wait()
+    couple_high[...], couple_low[...] = halves(couple_ref[...])
     relayout(0, even, 0)
     spread(left_ref, even, 0, turn_even, *even_parts)
     load(1).wait()
@@ -225,8 +224,8 @@
     zero_right = send(asc.at[1], other.at[1], zero_send.at[1], zero_recv.at[1], (partners[0], r))
     envs[0] = asc[0].astype(f32) + asc[1].astype(f32)
     def climb(level, partner):
-        couple = couple_ref[...]
-        carried = exact_turned(exact(couple, partner.reshape(square)), couple)
+        couple = (couple_high[...], couple_low[...])
+        carried = product(halves(product(couple, halves(partner.reshape(square)))), couple, turned_mm)
         envs[level + 1] = 0.5 * (envs[level] + carried.reshape(cut))
 
     with jax.named_scope('w_zero'):
@@ -265,10 +264,13 @@
                 grams[1] += mm(turned, rows)
         return carry
 
-    shares = 2 * (levels - 1) - 1
+    weights = [1, 1] * (levels - 1)
+    weights[0] = 0
+    weights[-2] = 2
+    bounds = [sum(weights[:n]) * half // sum(weights) for n in range(len(weights) + 1)]
 
     def gram_share(n):
-        lax.fori_loop(n * half // shares, (n + 1) * half // shares, gram_pass, 0)
+        lax.fori_loop(bounds[n], bounds[n + 1], gram_pass, 0)
 
     for level in range(1, levels):
         if level == 1:
@@ -277,7 +279,7 @@
         else:
             direct = send_direct(level)
             with jax.named_scope('slot_a'):
-                gram_share(2 * level - 3)
+                gram_share(2 * level - 2)
         with jax.named_scope('w_dir'):
             direct[0].wait_recv()
         passed = [
@@ -290,7 +292,7 @@
             with jax.named_scope('w_mix'):
                 arrived(gathered_mix)
         with jax.named_scope('slot_b'):
-            gram_share(2 * level - 2)
+            gram_share(2 * level - 1)
         with jax.named_scope('w_dir1'):
             direct[1].wait_recv()
         with jax.named_scope('w_fw'):
@@ -300,8 +302,10 @@
 
     env = envs[levels].reshape(square)
     top = env.astype(bf16)
-    wide = top.astype(f32)
-    crossed = exact(grams[1] + 0.5 * exact(wide.T, grams[2]), wide)
+    flip = top.T
+    high, low = halves(grams[2])
+    high, low = halves(grams[1] + 0.5 * (mm(flip, high) + mm(flip, low)))
+    crossed = mm(high, top) + mm(low, top)
     gram = grams[0] + crossed + crossed.T
     low = chi // 2
     packed[r] = jnp.concatenate([gram[:low], gram[low:, low:]], axis=1).astype(bf16)
@@ -314,92 +318,70 @@
             packed.at[r], packed.at[r], gr_send.at[mask - 1], gr_recv.at[mask - 1], device))
         gathered_gram.append(send(
             traces.at[r], traces.at[r], tr_send.at[mask - 1], tr_recv.at[mask - 1], device))
-    tails = [pltpu.make_async_copy(envs.at[levels], env_out, tail_sem.at[0])]
-    tails[0].start()
+    env_out[...] = envs[levels]
 
     def grad_pass(i, carry):
         mix = mixed[...].reshape(square)
         for n, src in enumerate((even, odd)):
-            for first in range(0, SLAB, GROUP):
-                mats = [src[i, first + j] for j in range(GROUP)]
-                rows = jnp.concatenate(mats, axis=0)
-                moved = jnp.concatenate([mm(mix, one) for one in mats], axis=0)
-                grad[2 * i + n, first:first + GROUP] = (moved + mm(rows, top)).reshape(GROUP, *square)
-            pltpu.make_async_copy(
-                grad.at[2 * i + n], grad_out.at[2 * i + n], grad_sem.at[2 * i + n]
-            ).start()
+            moved = jnp.concatenate([mm(mix, src[i, j]) for j in range(SLAB)], axis=0)
+            whole = moved + mm(src[i].reshape(SLAB * chi, chi), top)
+            grad_out[2 * i + n] = jnp.transpose(whole.reshape(SLAB, chi, chi), (1, 0, 2))
         return carry
 
     with jax.named_scope('grad'):
         lax.fori_loop(0, half, grad_pass, 0)
     with jax.named_scope('w_gram'):
         arrived(gathered_gram)
-    for n, (src, dst) in enumerate(((packed, gram_out), (traces, trace_out))):
-        tails.append(pltpu.make_async_copy(src, dst, tail_sem.at[n + 1]))
-        tails[-1].start()
-    for copy in tails:
-        copy.wait()
-    for c in range(chunks):
-        pltpu.make_async_copy(grad.at[c], grad_out.at[c], grad_sem.at[c]).wait()
+    gram_out[...] = packed[...]
+    trace_out[...] = traces[...]
     for copy in pending:
         copy.wait_send()
 
 
 def update_kernel(
-    grad_ref, env_ref, gram_ref, trace_ref, out_ref, env_out,
-    grads, env, grams, traces, held, in_sem, out_sem, tail_sem,
+    grads, env_ref, gram_ref, trace_ref, out_ref, env_out, held, out_sem, env_sem
 ):
-    def load(c):
-        return pltpu.make_async_copy(grad_ref.at[c], grads.at[c], in_sem.at[c])
-
-    gram_copy = pltpu.make_async_copy(gram_ref, grams, tail_sem.at[0])
-    trace_copy = pltpu.make_async_copy(trace_ref, traces, tail_sem.at[1])
-    env_in = pltpu.make_async_copy(env_ref, env, tail_sem.at[2])
-    env_back = pltpu.make_async_copy(env, env_out, tail_sem.at[3])
-    gram_copy.start()
-    trace_copy.start()
-    for c in range(grads.shape[0]):
-        load(c).start()
-    env_in.start()
+    env_back = pltpu.make_async_copy(env_ref, env_out, env_sem)
+    env_back.start()
     chi = out_ref.shape[0]
     low = chi // 2
-    gram_copy.wait()
-    trace_copy.wait()
-    packed = grams[0].astype(f32)
-    squares = traces[0]
-    for rank in range(1, grams.shape[0]):
-        packed = packed + grams[rank].astype(f32)
-        squares = squares + traces[rank]
+    packed = gram_ref[0].astype(f32)
+    squares = trace_ref[0]
+    for rank in range(1, gram_ref.shape[0]):
+        packed = packed + gram_ref[rank].astype(f32)
+        squares = squares + trace_ref[rank]
     scale = lax.rsqrt(squares[0:1, 0:1] + 1e-06)
     under = jnp.concatenate([packed[:, low:chi].T, packed[:, chi:]], axis=1)
     gram = jnp.concatenate([packed[:, :chi], under], axis=0) * (scale * scale)
     eye = diagonal(gram.shape).astype(f32)
-    twice = exact(gram, gram)
+    parts = halves(gram)
+    twice = product(parts, parts)
     bend = 1.6875 * eye - 0.5625 * gram + 0.0625 * twice
-    total = 2.25 * eye - 2.4375 * gram + exact(twice, bend)
+    total = 2.25 * eye - 2.4375 * gram + product(halves(twice), halves(bend))
     energy = jnp.sum(gram * eye, keepdims=True)
     mean = jnp.sum(gram * total, keepdims=True) / jnp.maximum(energy, 1e-30)
     rest = ((total - mean * eye) * scale).astype(bf16)
     mean = mean * scale
 
     def finish(c, carry):
-        load(c).wait()
         grad = grads[c].reshape(SLAB * chi, chi)
         done = (mean * grad + mm(grad.astype(bf16), rest)).astype(bf16)
-        held[c] = jnp.transpose(done.reshape(SLAB, chi, chi), (1, 0, 2))
+        held[c] = done.reshape(chi, SLAB, chi)
         pltpu.make_async_copy(
             held.at[c], out_ref.at[:, pl.ds(pl.multiple_of(c * SLAB, SLAB), SLAB), :], out_sem.at[c]
         ).start()
         return carry
 
     lax.fori_loop(0, held.shape[0], finish, 0)
-    env_in.wait()
-    env_back.start()
     for c in range(held.shape[0]):
         pltpu.make_async_copy(
             held.at[c], out_ref.at[:, pl.ds(c * SLAB, SLAB), :], out_sem.at[c]
         ).wait()
     env_back.wait()
+
+
+def in_hbm(array):
+    return pltpu.with_memory_space_constraint(array, pltpu.HBM)
 
 
 def body(iso, edge_left, edge_right, coupling):
@@ -414,22 +396,24 @@
     half = chunks // 2
     work = 2 * depth * chi**3
     dma = pltpu.SemaphoreType.DMA
+    vmem = pl.BlockSpec(memory_space=pltpu.VMEM)
     hbm = pl.BlockSpec(memory_space=pltpu.HBM)
     grad, environ, grams, traces = pl.pallas_call(
         functools.partial(sweep_kernel, blk, bond, levels),
         in_specs=[hbm] * 4,
-        out_specs=[hbm] * 4,
+        out_specs=[vmem] * 4,
         out_shape=[
-            jax.ShapeDtypeStruct((chunks, SLAB, *square), f32),
-            jax.ShapeDtypeStruct((bond, piece, chi), f32),
-            jax.ShapeDtypeStruct((bond, chi // 2, chi + chi // 2), bf16),
-            jax.ShapeDtypeStruct((bond, 8, 128), f32),
+            pltpu.VMEM((chunks, chi, SLAB, chi), f32),
+            pltpu.VMEM((bond, piece, chi), f32),
+            pltpu.VMEM((bond, chi // 2, chi + chi // 2), bf16),
+            pltpu.VMEM((bond, 8, 128), f32),
         ],
         scratch_shapes=[
             pltpu.VMEM(square, bf16),
             pltpu.VMEM(square, bf16),
             pltpu.VMEM(square, f32),
-            pltpu.VMEM((chunks, SLAB, *square), f32),
+            pltpu.VMEM(square, bf16),
+            pltpu.VMEM(square, bf16),
             pltpu.VMEM((min(4, chunks), chi, SLAB, chi), bf16),
             pltpu.VMEM((half + 1, SLAB, *square), bf16),
             pltpu.VMEM((half + 1, SLAB, *square), bf16),
@@ -450,7 +434,7 @@
             pltpu.VMEM((3, *square), f32),
             pltpu.VMEM((bond, chi // 2, chi + chi // 2), bf16),
             pltpu.VMEM((bond, 8, 128), f32),
-            dma((min(4, chunks),)), dma((3,)), dma((chunks,)), dma((3,)),
+            dma((min(4, chunks),)), dma((3,)),
             dma((2, bond - 1)), dma((2, bond - 1)),
             dma((2, bond - 1)), dma((2, bond - 1)),
             dma((2,)), dma((2,)), dma((2,)), dma((2,)),
@@ -465,23 +449,16 @@
         ),
         cost_estimate=pl.CostEstimate(flops=10 * work, bytes_accessed=4 * iso.size, transcendentals=0),
         name="sweep",
-    )(iso, edge_left[0], edge_right[0], coupling[0])
+    )(*map(in_hbm, (iso, edge_left[0], edge_right[0], coupling[0])))
     updated, environ = pl.pallas_call(
         update_kernel,
-        in_specs=[hbm] * 4,
+        in_specs=[vmem] * 4,
         out_specs=[hbm] * 2,
         out_shape=[
             jax.ShapeDtypeStruct(iso.shape, bf16),
             jax.ShapeDtypeStruct((bond, piece, chi), f32),
         ],
-        scratch_shapes=[
-            pltpu.VMEM((chunks, SLAB, *square), f32),
-            pltpu.VMEM((bond, piece, chi), f32),
-            pltpu.VMEM((bond, chi // 2, chi + chi // 2), bf16),
-            pltpu.VMEM((bond, 8, 128), f32),
-            pltpu.VMEM((chunks, chi, SLAB, chi), bf16),
-            dma((chunks,)), dma((chunks,)), dma((4,)),
-        ],
+        scratch_shapes=[pltpu.VMEM((chunks, chi, SLAB, chi), bf16), dma((chunks,)), dma],
         compiler_params=pltpu.CompilerParams(vmem_limit_bytes=UPDATE_VMEM),
         cost_estimate=pl.CostEstimate(flops=work, bytes_accessed=4 * iso.size, transcendentals=0),
         name="update",

time: 77.7 us -> 67.8 us (0.87)
  Pallas kernels: 76.7 us -> 66.8 us
    pallas_call x1, Pallas kernels: 12.5 us -> 5.54 us  [body(): pl.pallas_call(update_kernel, in_specs=[vmem] * 4, out_specs=[hbm] * 2, o...]
    pallas_call x1, Pallas kernels: 64.2 us -> 61.2 us  [body(): pl.pallas_call(functools.partial(sweep_kernel, blk, bond, levels), in_spe...]
where the time goes in v3:
time: 67.8 us; the launch traced here: 67.6 us
  Pallas kernels  66.8 us (99%)
  between operations  0.8 us (1%)
    pallas_call x1, Pallas kernels, body(): pl.pallas_call(functools.partial(sweep_kernel, blk, bond, levels), in_spe...  61.2 us
    pallas_call x1, Pallas kernels, body(): pl.pallas_call(update_kernel, in_specs=[vmem] * 4, out_specs=[hbm] * 2, o...  5.54 us

profile of v3, /device:TPU:0, one launch (start us, length us, event | category | flops | bytes accessed | tf_op | source)
XLA Modules:
  0.0 67.6 jit_solution(8062908006181526884)
XLA Ops:
  0.6 61.2 %sweep.1 = (f32[8,256,8,256]{3,2,1,0:T(8,128)S(1)}, f32[4,64,256]{2,1,0:T(8,128)S(1)}, bf16[4,128,384]{2,1,0:T(8,128)(2,1)S(1)}, f32[4,8,128]{2,1,0:T(8,128)S(1)}) custom-call(bf16[256,64,256]{2,1,0:T(8,128)(2,1)} %bitcast.6, bf16[256,256]{1,0:T(8,128)(2,1)} %bitcast.10, bf16[256,256]{1,0:T(8,128)(2,1)} %bitcast.11, f32[256,256]{1,0:T(8,128)} %bitcast.8), custom_call_target="tpu_custom_call" | custom-call | flops 21474836480 | bytes 16777216 | tf_op jit(solution)/shard_map/sweep/pallas_call | solution.py:401
  61.9 5.5 %update.1 = (bf16[256,64,256]{2,1,0:T(8,128)(2,1)}, f32[4,64,256]{2,1,0:T(8,128)}) custom-call(f32[8,256,8,256]{3,2,1,0:T(8,128)S(1)} %get-tuple-element.8.grads, f32[4,64,256]{2,1,0:T(8,128)S(1)} %get-tuple-element.9.env_ref, bf16[4,128,384]{2,1,0:T(8,128)(2,1)S(1)} %get-tuple-element.10.gram_ref, f32[4,8,128]{2,1,0:T(8,128)S(1)} %get-tuple-element.11.trace_ref), custom_call_target="tpu_custom_call" | custom-call | flops 2147483648 | bytes 16777216 | tf_op jit(solution)/shard_map/update/pallas_call | solution.py:453

commit v4 on v3

--- a/solution.py
+++ b/solution.py
@@ -69,7 +69,7 @@
     cut = (bond, piece, chi)
     after = lax.rem(s + 1, blk)
     before = lax.rem(s + blk - 1, blk)
-    masks = range(1, bond)
+    masks = range(bond - 1, 0, -1)
     pending = []
 
     def load(c):

time: 67.8 us -> 67.1 us (0.990)
  no operation moved by 1% of the time
where the time goes in v4:
time: 67.1 us; the launch traced here: 67 us
  Pallas kernels  66.2 us (99%)
  between operations  0.8 us (1%)
    pallas_call x1, Pallas kernels, body(): pl.pallas_call(functools.partial(sweep_kernel, blk, bond, levels), in_spe...  60.6 us
    pallas_call x1, Pallas kernels, body(): pl.pallas_call(update_kernel, in_specs=[vmem] * 4, out_specs=[hbm] * 2, o...  5.55 us

profile of v4, /device:TPU:0, one launch (start us, length us, event | category | flops | bytes accessed | tf_op | source)
XLA Modules:
  0.0 67.0 jit_solution(17801333541111699284)
XLA Ops:
  0.6 60.6 %sweep.1 = (f32[8,256,8,256]{3,2,1,0:T(8,128)S(1)}, f32[4,64,256]{2,1,0:T(8,128)S(1)}, bf16[4,128,384]{2,1,0:T(8,128)(2,1)S(1)}, f32[4,8,128]{2,1,0:T(8,128)S(1)}) custom-call(bf16[256,64,256]{2,1,0:T(8,128)(2,1)} %bitcast.6, bf16[256,256]{1,0:T(8,128)(2,1)} %bitcast.10, bf16[256,256]{1,0:T(8,128)(2,1)} %bitcast.11, f32[256,256]{1,0:T(8,128)} %bitcast.8), custom_call_target="tpu_custom_call" | custom-call | flops 21474836480 | bytes 16777216 | tf_op jit(solution)/shard_map/sweep/pallas_call | solution.py:401
  61.3 5.5 %update.1 = (bf16[256,64,256]{2,1,0:T(8,128)(2,1)}, f32[4,64,256]{2,1,0:T(8,128)}) custom-call(f32[8,256,8,256]{3,2,1,0:T(8,128)S(1)} %get-tuple-element.8.grads, f32[4,64,256]{2,1,0:T(8,128)S(1)} %get-tuple-element.9.env_ref, bf16[4,128,384]{2,1,0:T(8,128)(2,1)S(1)} %get-tuple-element.10.gram_ref, f32[4,8,128]{2,1,0:T(8,128)S(1)} %get-tuple-element.11.trace_ref), custom_call_target="tpu_custom_call" | custom-call | flops 2147483648 | bytes 16777216 | tf_op jit(solution)/shard_map/update/pallas_call | solution.py:453
